TPU v7x, 32 devices: a whole 2x2x4 slice. The times are simulated.
32 devices in a mesh: ep: 8 (over z, x), etp: 4 (over y, core).
Axes of the slice: x: 2, y: 2, z: 4, core: 2. Of those that a mesh axis runs over, the one named last changes fastest.
Arguments:
- tokens: bfloat16 [1024, 4096], P('ep', 'etp'), may hold values from -6 to 6
- expert_ids: int32 [1024, 8], P('ep'), may hold values from 0 to 15, all different within a row; in each aligned block of 128 rows (0 to 127, 128 to 255, ...) at most 96 rows name the same one
- gate_prob: float32 [1024, 8], P('ep'), may hold values from 0.05 to 1
- gate_weight: bfloat16 [16, 4096, 1536], P('ep', None, 'etp'), may hold values from -0.09375 to 0.09375
- up_weight: bfloat16 [16, 4096, 1536], P('ep', None, 'etp'), may hold values from -0.09375 to 0.09375
- down_weight: bfloat16 [16, 1536, 4096], P('ep', 'etp'), may hold values from -0.15625 to 0.15625
Outputs:
- mixed: bfloat16 [1024, 4096], P('ep', 'etp')
Inputs may be any that keep to these rules, and one draw needn't show every extreme that they name: `expert_ids`: each row names 8 different experts. Within each aligned block of 128 rows (one token group) no expert is named more than 96 times, and in every draw some expert is named exactly 96 times in some block.
All inputs are finite; a program needn't handle non-finite values.
Results may differ from a plain program's by a relative error of at most 0.012.
Values may be sent and summed in bfloat16 or wider, within the bound.
A program may use at most 128 MiB of HBM per device.

v0:
```python
from functools import partial
import jax
import jax.numpy as jnp
from jax import lax
from jax.sharding import PartitionSpec as P


def add_features(totals, portion, offset, w_gate, w_up):
    return (
        jnp.dot(portion, w_gate, preferred_element_type=jnp.float32),
        jnp.dot(portion, w_up, preferred_element_type=jnp.float32),
    )


def body(tokens, expert_ids, gate_prob, gate_weight, up_weight, down_weight):
    groups = lax.axis_size("ep")
    local_experts = gate_weight.shape[0]
    experts = local_experts * groups
    tok_rows = expert_ids.shape[0]
    fanout = expert_ids.shape[1]
    capacity = max(2, 3 * tok_rows * fanout // (2 * experts))
    flat_ids = expert_ids.reshape(-1)
    onehot = (flat_ids[:, None] == jnp.arange(experts, dtype=jnp.int32)[None, :]).astype(jnp.int32)
    position = jnp.sum((jnp.cumsum(onehot, axis=0) - onehot) * onehot, axis=1)
    slot_index = flat_ids * capacity + position
    owners = jnp.arange(tok_rows * fanout, dtype=jnp.int32) // fanout
    source = jnp.full((experts * capacity,), tok_rows, jnp.int32).at[slot_index].set(owners)
    padded = jnp.concatenate([tokens, jnp.zeros((1, tokens.shape[1]), tokens.dtype)], axis=0)
    outgoing = padded[source].reshape(groups, local_experts, capacity, tokens.shape[1])
    arrived = lax.all_to_all(outgoing, "ep", split_axis=0, concat_axis=2, tiled=True)
    partials = []
    for member in range(local_experts):
        expert_rows = arrived[0, member]
        starting = jnp.zeros((expert_rows.shape[0], gate_weight.shape[2]), jnp.float32)
        folder = partial(add_features, w_gate=gate_weight[member], w_up=up_weight[member])
        gate_sum, up_sum = folder(
            (starting, starting),
            lax.all_gather(expert_rows, "etp", axis=1, tiled=True),
            jnp.int32(0),
        )
        hidden = (jax.nn.silu(gate_sum) * up_sum).astype(jnp.bfloat16)
        partials.append(jnp.dot(hidden, down_weight[member], preferred_element_type=jnp.float32))
    partial_all = jnp.stack(partials).reshape(local_experts, groups, capacity, down_weight.shape[2])
    combine_scale = gate_prob.reshape(tok_rows, fanout, 1)
    summed = lax.psum_scatter(
        partial_all.astype(jnp.bfloat16), "etp", scatter_dimension=3, tiled=True
    ).astype(jnp.float32)
    returned = lax.all_to_all(
        summed.astype(jnp.bfloat16), "ep", split_axis=1, concat_axis=0, tiled=True
    ).astype(summed.dtype)
    picked = returned.reshape(experts * capacity, -1)[slot_index].reshape(tok_rows, fanout, -1)
    mixed = jnp.sum(picked * combine_scale, axis=1).astype(jnp.bfloat16)
    return mixed


def solution(mesh):
    in_specs = (
        P("ep", "etp"),
        P("ep", None),
        P("ep", None),
        P("ep", None, "etp"),
        P("ep", None, "etp"),
        P("ep", "etp", None),
    )
    out_specs = P("ep", "etp")
    return jax.shard_map(body, mesh=mesh, in_specs=in_specs, out_specs=out_specs, check_vma=False)
```

profile of v0, /device:TPU:0, one launch (start us, length us, event | category | flops | bytes accessed | tf_op | source)
XLA Modules:
  0.0 419.7 jit_solution(9803007199391855178)
XLA Ops:
  6.5 0.8 copy.19
  8.2 4.5 %reduce-window.6 = s32[16,8,128]{2,1,0:T(8,128)S(1)} reduce-window(s32[16,8,128]{2,1,0:T(8,128)S(1)} %fusion.46, s32[]{:T(128)} %constant.32.clone.1), window={size=1x1x128 pad=0_0x0_0x127_0}, to_apply=%region_0.0 | reduce-window | flops 2080768 | bytes 131076 | tf_op jit(solution)/shard_map/reduce-window
  13.4 4.3 %scatter_custom_fusion = s32[1536]{0:T(1024)S(1)} fusion(s32[1024]{0:T(1024)S(1)} %bitcast.98, s32[1024]{0:T(1024)S(1)} %add_select_fusion, s32[]{:T(128)} %constant.30.clone.1), kind=kCustom, calls=%fused_computation.52 | custom fusion | bytes 6148 | tf_op jit(solution)/shard_map/scatter | solution.py:27
  17.7 1.0 concatenate.5
  18.7 5.1 %gather_fusion = bf16[1536,1024]{1,0:T(8,128)(2,1)S(1)} fusion(bf16[129,1024]{1,0:T(8,128)(2,1)S(1)} %concatenate.5, s32[2048]{0:T(1024)S(1)} %pad_clamp_fusion), kind=kCustom, calls=%fused_computation | custom fusion | bytes 6297600 | tf_op jit(solution)/shard_map/gather | solution.py:29
  23.8 77.8 %all_to_all.27 = bf16[8,2,96,1024]{3,2,1,0:T(8,128)(2,1)S(1)} all-to-all(bf16[8,2,96,1024]{3,2,1,0:T(8,128)(2,1)S(1)} %bitcast.92), channel_id=1, replica_groups=mesh['ep'=8,'etp'=4] {'ep'}, dimensions={0} | all-to-all | bytes 6291456 | tf_op jit(solution)/shard_map/all_to_all | solution.py:30
  102.0 1.9 fusion.52
  104.0 0.7 all-gather.7.cloned.1.call-update
  105.0 44.6 %all-gather.5.cloned.1.call-done = bf16[1,1,768,4096]{3,2,1,0:T(8,128)(2,1)} async-done(((bf16[1,1,768,1024]{3,2,1,0:T(8,128)(2,1)}), bf16[1,1,768,4096]{3,2,1,0:T(8,128)(2,1)}) %all-gather.5.cloned.1.call-update) | async-done | bytes 6291472 | tf_op jit(solution)/shard_map/all_gather | solution.py:38
  149.5 6.6 %fusion.6 = f32[768,384]{1,0:T(8,128)S(1)} fusion(bf16[1,1,768,4096]{3,2,1,0:T(8,128)(2,1)} %all-gather.5.cloned.1.call-done, bf16[2,4096,384]{2,1,0:T(8,128)(2,1)} %param.9), kind=kOutput, calls=%fused_computation.12 | convolution fusion | flops 2415919104 | bytes 10616832 | tf_op jit(solution)/shard_map/dot_general | solution.py:10
  156.1 5.9 %fusion.38 = bf16[768,384]{1,0:T(8,128)(2,1)S(1)} fusion(bf16[2,4096,384]{2,1,0:T(8,128)(2,1)} %param.10, bf16[1,1,768,4096]{3,2,1,0:T(8,128)(2,1)S(1)} %copy-done.1, f32[768,384]{1,0:T(8,128)S(1)} %fusion.6), kind=kOutput, calls=%fused_computation.34 | convolution fusion | flops 2417688576 | bytes 11206656 | tf_op jit(solution)/shard_map/dot_general | solution.py:11
  162.0 5.4 %fusion.8 = bf16[1,8,96,4096]{3,2,1,0:T(8,128)(2,1)} fusion(bf16[8,96,384]{2,1,0:T(8,128)(2,1)S(1)} %bitcast.104, bf16[2,384,4096]{2,1,0:T(8,128)(2,1)S(1)} %bitcast.101), kind=kOutput, calls=%fused_computation.14 | convolution fusion | flops 2419064832 | bytes 10027008 | tf_op jit(solution)/shard_map/dot_general | solution.py:42
  167.4 30.1 %all-gather.7.cloned.1.call-done = bf16[1,1,768,4096]{3,2,1,0:T(8,128)(2,1)} async-done(((bf16[1,1,768,1024]{3,2,1,0:T(8,128)(2,1)}), bf16[1,1,768,4096]{3,2,1,0:T(8,128)(2,1)}) %all-gather.7.cloned.1.call-update) | async-done | bytes 6291472 | tf_op jit(solution)/shard_map/all_gather | solution.py:38
  197.5 6.6 %fusion.2 = f32[768,384]{1,0:T(8,128)S(1)} fusion(bf16[1,1,768,4096]{3,2,1,0:T(8,128)(2,1)} %all-gather.7.cloned.1.call-done, bf16[2,4096,384]{2,1,0:T(8,128)(2,1)} %param.9), kind=kOutput, calls=%fused_computation.8 | convolution fusion | flops 2415919104 | bytes 10616832 | tf_op jit(solution)/shard_map/dot_general | solution.py:10
  204.1 5.7 %fusion.33 = bf16[768,384]{1,0:T(8,128)(2,1)S(1)} fusion(bf16[2,4096,384]{2,1,0:T(8,128)(2,1)} %param.10, bf16[1,1,768,4096]{3,2,1,0:T(8,128)(2,1)S(1)} %copy-done.2, f32[768,384]{1,0:T(8,128)S(1)} %fusion.2), kind=kOutput, calls=%fused_computation.33 | convolution fusion | flops 2417688576 | bytes 11206656 | tf_op jit(solution)/shard_map/dot_general | solution.py:11
  209.9 3.6 fusion.9
  213.5 5.3 %pad_maximum_fusion = bf16[2,8,96,4096]{3,2,1,0:T(8,128)(2,1)} fusion(bf16[1,8,96,4096]{3,2,1,0:T(8,128)(2,1)S(1)} %fusion.9, bf16[1,8,96,4096]{3,2,1,0:T(8,128)(2,1)S(1)} %bitcast.94), kind=kLoop, calls=%fused_computation.3 | loop fusion | flops 6291456 | bytes 25165824 | tf_op jit(solution)/shard_map/stack | solution.py:43
  218.8 97.3 %reduce-scatter.2.cloned.1.call-done = bf16[2,8,96,1024]{3,2,1,0:T(8,128)(2,1)} async-done(((bf16[2,8,96,4096]{3,2,1,0:T(8,128)(2,1)}), bf16[2,8,96,1024]{3,2,1,0:T(8,128)(2,1)}) %reduce-scatter.2.cloned.1.call-update) | async-done | bytes 3145744 | tf_op jit(solution)/shard_map/reduce_scatter | solution.py:45
  316.1 3.9 copy.24
  320.1 5.6 %all-to-all-start.1 = ((bf16[2,8,96,1024]{3,2,0,1:T(8,128)(2,1)}), bf16[2,8,96,1024]{3,2,0,1:T(8,128)(2,1)S(1)}, u32[]{:S(2)}, u32[]{:S(2)}) async-start(bf16[2,8,96,1024]{3,2,0,1:T(8,128)(2,1)} %copy.24), calls=%async_computation.2 | async-start | bytes 6291456 | tf_op jit(solution)/shard_map/all_to_all | solution.py:48
  325.8 70.4 %all-to-all-done.1 = bf16[2,8,96,1024]{3,2,0,1:T(8,128)(2,1)S(1)} async-done(((bf16[2,8,96,1024]{3,2,0,1:T(8,128)(2,1)}), bf16[2,8,96,1024]{3,2,0,1:T(8,128)(2,1)S(1)}, u32[]{:S(2)}, u32[]{:S(2)}) %all-to-all-start.1) | async-done | bytes 3145760 | tf_op jit(solution)/shard_map/all_to_all | solution.py:48
  396.3 3.4 bitcast_convert_fusion
  399.7 9.3 %gather_fusion.1 = f32[1024,1024]{1,0:T(8,128)} fusion(f32[1536,1024]{1,0:T(8,128)} %bitcast.90, s32[1024]{0:T(1024)S(1)} %broadcast_clamp_fusion), kind=kCustom, calls=%fused_computation.1 | custom fusion | bytes 8392704 | tf_op jit(solution)/shard_map/gather | solution.py:51
  409.0 4.2 fusion.10
  (46 shorter events, 2.4 us)
Async XLA Ops:
  6.5 143.0 %all-gather.5.cloned.1.call-start = ((), (), s32[]{:S(2)}) async-start(), calls=%async_computation.4 | async-start | bytes 7864320 | tf_op jit(solution)/shard_map/all_gather | solution.py:38
  104.0 93.5 %all-gather.7.cloned.1.call-start = ((), (), s32[]{:S(2)}) async-start(), calls=%async_computation.5 | async-start | bytes 7864320 | tf_op jit(solution)/shard_map/all_gather | solution.py:38
  104.7 211.4 %reduce-scatter.2.cloned.1.call-start = ((), (), s32[]{:S(2)}) async-start(), calls=%async_computation.3 | async-start | bytes 15728640 | tf_op jit(solution)/shard_map/reduce_scatter | solution.py:45
  149.5 6.6 %copy-start.1 = (bf16[1,1,768,4096]{3,2,1,0:T(8,128)(2,1)S(1)}, bf16[1,1,768,4096]{3,2,1,0:T(8,128)(2,1)}, u32[]{:S(2)}) copy-start(bf16[1,1,768,4096]{3,2,1,0:T(8,128)(2,1)} %all-gather.5.cloned.1.call-done) | copy-start | bytes 18874372
  149.5 12.5 %slice-start.2 = ((s8[6291456]{0:T(1024)(128)(4,1)}), s8[4194304]{0:T(1024)(128)(4,1)S(1)}, s32[]{:S(2)}) async-start(s8[6291456]{0:T(1024)(128)(4,1)} %bitcast.100), calls=%async_computation.8 | async-start | bytes 8388608
  156.1 5.9 %slice-start.3 = ((s8[6291456]{0:T(1024)(128)(4,1)}), s8[2097152]{0:T(1024)(128)(4,1)S(1)}, s32[]{:S(2)}) async-start(s8[6291456]{0:T(1024)(128)(4,1)} %bitcast.100), calls=%async_computation.9 | async-start | bytes 4194304
  197.5 6.6 %copy-start.2 = (bf16[1,1,768,4096]{3,2,1,0:T(8,128)(2,1)S(1)}, bf16[1,1,768,4096]{3,2,1,0:T(8,128)(2,1)}, u32[]{:S(2)}) copy-start(bf16[1,1,768,4096]{3,2,1,0:T(8,128)(2,1)} %all-gather.7.cloned.1.call-done) | copy-start | bytes 18874372
  197.5 12.4 %slice-start.4 = ((s8[6291456]{0:T(1024)(128)(4,1)}), s8[4194304]{0:T(1024)(128)(4,1)S(1)}, s32[]{:S(2)}) async-start(s8[6291456]{0:T(1024)(128)(4,1)} %bitcast.102), calls=%async_computation.10 | async-start | bytes 8388608
  197.5 16.0 %slice-start = ((s8[6291456]{0:T(1024)(128)(4,1)}), s8[4194304]{0:T(1024)(128)(4,1)S(1)}, s32[]{:S(2)}) async-start(s8[6291456]{0:T(1024)(128)(4,1)} %bitcast.93), calls=%async_computation.6 | async-start | bytes 8388608
  204.1 5.8 %slice-start.5 = ((s8[6291456]{0:T(1024)(128)(4,1)}), s8[2097152]{0:T(1024)(128)(4,1)S(1)}, s32[]{:S(2)}) async-start(s8[6291456]{0:T(1024)(128)(4,1)} %bitcast.102), calls=%async_computation.11 | async-start | bytes 4194304
  204.1 9.4 %slice-start.1 = ((s8[6291456]{0:T(1024)(128)(4,1)}), s8[2097152]{0:T(1024)(128)(4,1)S(1)}, s32[]{:S(2)}) async-start(s8[6291456]{0:T(1024)(128)(4,1)} %bitcast.93), calls=%async_computation.7 | async-start | bytes 4194304
  320.1 5.6 %copy-start = (f32[128,8]{0,1:T(8,128)S(1)}, f32[128,8]{0,1:T(8,128)}, u32[]{:S(2)}) copy-start(f32[128,8]{0,1:T(8,128)} %param.8) | copy-start | bytes 12292
  320.1 76.2 %all-to-all-start.1 = ((bf16[2,8,96,1024]{3,2,0,1:T(8,128)(2,1)}), bf16[2,8,96,1024]{3,2,0,1:T(8,128)(2,1)S(1)}, u32[]{:S(2)}, u32[]{:S(2)}) async-start(bf16[2,8,96,1024]{3,2,0,1:T(8,128)(2,1)} %copy.24), calls=%async_computation.2 | async-start | bytes 6291456 | tf_op jit(solution)/shard_map/all_to_all | solution.py:48
Sparse Core Ops, SparseCore 0:
  104.1 45.3 all-gather.4
  151.1 46.3 all-gather.6
  219.0 97.1 reduce-scatter.1
where the time goes:
time: 420 us
  waiting for transfers between devices  243 us (58%)
  blocking collectives  77.8 us (19%)
  matrix products  33.8 us (8%)
  local copies, waits for them, and re-layouts  27.5 us (7%)
  other arithmetic  18.3 us (4%)
  between operations  13.3 us (3%)
  starting transfers between devices  5.9 us (1%)
    reduce_scatter x1, waiting for transfers between devices, body(): lax.psum_scatter(partial_all.astype(jnp.bfloat16), 'etp', scatter_dimensi...  97.3 us
    all_to_all x1, blocking collectives, body(): lax.all_to_all(outgoing, 'ep', split_axis=0, concat_axis=2, tiled=True)  77.8 us
    all_gather x2, waiting for transfers between devices, body(): lax.all_gather(expert_rows, 'etp', axis=1, tiled=True)  74.6 us
    all_to_all x1, waiting for transfers between devices, body(): lax.all_to_all(summed.astype(jnp.bfloat16), 'ep', split_axis=1, concat_ax...  70.4 us
    dot_general x2, matrix products, add_features(): jnp.dot(portion, w_gate, preferred_element_type=jnp.float32)  13.1 us
    dot_general x2, matrix products, add_features(): jnp.dot(portion, w_up, preferred_element_type=jnp.float32)  11.6 us
    gather x1, local copies, waits for them, and re-layouts, body(): returned.reshape(experts * capacity, -1)[slot_index]  9.27 us
    dot_general x2, matrix products, body(): jnp.dot(hidden, down_weight[member], preferred_element_type=jnp.float32)  9 us
  transfers between devices with their start and end apart: 4, of which 4 were waited for; matrix products, arithmetic and copies ran while one was open for 4% of the time, Pallas kernels for 0%

commit v1 on v0

--- a/solution.py
+++ b/solution.py
@@ -3,6 +3,11 @@
 import jax.numpy as jnp
 from jax import lax
 from jax.sharding import PartitionSpec as P
+
+
+def all_parts(shard, axis, dim):
+    pieces = lax.all_gather(shard, axis)
+    return jnp.concatenate(pieces, axis=dim)
 
 
 def add_features(totals, portion, offset, w_gate, w_up):
@@ -34,9 +39,7 @@
         starting = jnp.zeros((expert_rows.shape[0], gate_weight.shape[2]), jnp.float32)
         folder = partial(add_features, w_gate=gate_weight[member], w_up=up_weight[member])
         gate_sum, up_sum = folder(
-            (starting, starting),
-            lax.all_gather(expert_rows, "etp", axis=1, tiled=True),
-            jnp.int32(0),
+            (starting, starting), all_parts(expert_rows, "etp", 1), jnp.int32(0)
         )
         hidden = (jax.nn.silu(gate_sum) * up_sum).astype(jnp.bfloat16)
         partials.append(jnp.dot(hidden, down_weight[member], preferred_element_type=jnp.float32))

time: 420 us -> 438 us (1.043)
  local copies, waits for them, and re-layouts: 27.5 us -> 44.9 us
    all_gather x0 -> x2, local copies, waits for them, and re-layouts: none -> 17.4 us  [all_parts(): pieces = lax.all_gather(shard, axis)]
where the time goes in v1:
time: 438 us
  waiting for transfers between devices  243 us (55%)
  blocking collectives  77.8 us (18%)
  local copies, waits for them, and re-layouts  44.9 us (10%)
  matrix products  34.6 us (8%)
  other arithmetic  18.3 us (4%)
  between operations  13.3 us (3%)
  starting transfers between devices  5.91 us (1%)
    reduce_scatter x1, waiting for transfers between devices, body(): lax.psum_scatter(partial_all.astype(jnp.bfloat16), 'etp', scatter_dimensi...  97.3 us
    all_to_all x1, blocking collectives, body(): lax.all_to_all(outgoing, 'ep', split_axis=0, concat_axis=2, tiled=True)  77.8 us
    all_gather x2, waiting for transfers between devices, all_parts(): pieces = lax.all_gather(shard, axis)  74.2 us
    all_to_all x1, waiting for transfers between devices, body(): lax.all_to_all(summed.astype(jnp.bfloat16), 'ep', split_axis=1, concat_ax...  70.4 us
    all_gather x2, local copies, waits for them, and re-layouts, all_parts(): pieces = lax.all_gather(shard, axis)  17.4 us
    dot_general x2, matrix products, add_features(): jnp.dot(portion, w_gate, preferred_element_type=jnp.float32)  16.3 us
    dot_general x2, matrix products, add_features(): jnp.dot(portion, w_up, preferred_element_type=jnp.float32)  11.1 us
    gather x1, local copies, waits for them, and re-layouts, body(): returned.reshape(experts * capacity, -1)[slot_index]  9.22 us
  transfers between devices with their start and end apart: 4, of which 4 were waited for; matrix products, arithmetic and copies ran while one was open for 4% of the time, Pallas kernels for 0%

profile of v1, /device:TPU:0, one launch (start us, length us, event | category | flops | bytes accessed | tf_op | source)
XLA Modules:
  0.0 437.6 jit_solution(13424729478029715407)
XLA Ops:
  8.2 4.5 %reduce-window.6 = s32[16,8,128]{2,1,0:T(8,128)S(1)} reduce-window(s32[16,8,128]{2,1,0:T(8,128)S(1)} %fusion.34, s32[]{:T(128)} %constant.32.clone.1), window={size=1x1x128 pad=0_0x0_0x127_0}, to_apply=%region_0.0 | reduce-window | flops 2080768 | bytes 131076 | tf_op jit(solution)/shard_map/reduce-window
  13.4 4.3 scatter_custom_fusion
  17.7 1.0 concatenate.5
  18.7 5.1 %gather_fusion = bf16[1536,1024]{1,0:T(8,128)(2,1)S(1)} fusion(bf16[129,1024]{1,0:T(8,128)(2,1)S(1)} %concatenate.5, s32[2048]{0:T(1024)S(1)} %pad_clamp_fusion), kind=kCustom, calls=%fused_computation | custom fusion | bytes 6297600 | tf_op jit(solution)/shard_map/gather | solution.py:34
  23.8 77.8 %all_to_all.27 = bf16[8,2,96,1024]{3,2,1,0:T(8,128)(2,1)S(1)} all-to-all(bf16[8,2,96,1024]{3,2,1,0:T(8,128)(2,1)S(1)} %bitcast.88), channel_id=1, replica_groups=mesh['ep'=8,'etp'=4] {'ep'}, dimensions={0} | all-to-all | bytes 6291456 | tf_op jit(solution)/shard_map/all_to_all | solution.py:35
  102.0 1.9 fusion.40
  105.0 44.6 %all-gather.5.cloned.1.call-done = bf16[4,1,768,1024]{3,2,1,0:T(8,128)(2,1)} async-done(((bf16[1,1,768,1024]{3,2,1,0:T(8,128)(2,1)}), bf16[4,1,768,1024]{3,2,1,0:T(8,128)(2,1)}) %all-gather.5.cloned.1.call-update) | async-done | bytes 6291472 | tf_op jit(solution)/shard_map/all_gather | solution.py:9
  149.5 8.7 %copy.26 = bf16[4,1,768,1024]{2,3,0,1:T(8,128)(2,1)} copy(bf16[4,1,768,1024]{3,2,1,0:T(8,128)(2,1)} %all-gather.5.cloned.1.call-done) | data formatting | bytes 12582912 | tf_op jit(solution)/shard_map/all_gather | solution.py:9
  158.2 9.6 %fusion.11 = f32[768,384]{1,0:T(8,128)} fusion(bf16[768,4096]{0,1:T(8,128)(2,1)} %bitcast.89, bf16[2,4096,384]{2,1,0:T(8,128)(2,1)} %param.9), kind=kOutput, calls=%fused_computation.19 | convolution fusion | flops 2415919104 | bytes 10616832 | tf_op jit(solution)/shard_map/dot_general | solution.py:15
  167.9 29.6 %all-gather.7.cloned.1.call-done = bf16[4,1,768,1024]{3,2,1,0:T(8,128)(2,1)} async-done(((bf16[1,1,768,1024]{3,2,1,0:T(8,128)(2,1)}), bf16[4,1,768,1024]{3,2,1,0:T(8,128)(2,1)}) %all-gather.7.cloned.1.call-update) | async-done | bytes 6291472 | tf_op jit(solution)/shard_map/all_gather | solution.py:9
  197.5 8.7 %copy.27 = bf16[4,1,768,1024]{2,3,0,1:T(8,128)(2,1)} copy(bf16[4,1,768,1024]{3,2,1,0:T(8,128)(2,1)} %all-gather.7.cloned.1.call-done) | data formatting | bytes 12582912 | tf_op jit(solution)/shard_map/all_gather | solution.py:9
  206.2 6.6 %fusion.6 = f32[768,384]{1,0:T(8,128)S(1)} fusion(bf16[768,4096]{0,1:T(8,128)(2,1)} %bitcast.93, bf16[2,4096,384]{2,1,0:T(8,128)(2,1)} %param.9), kind=kOutput, calls=%fused_computation.14 | convolution fusion | flops 2415919104 | bytes 10616832 | tf_op jit(solution)/shard_map/dot_general | solution.py:15
  212.9 5.5 %fusion.28 = bf16[768,384]{1,0:T(8,128)(2,1)S(1)} fusion(bf16[768,4096]{0,1:T(8,128)(2,1)S(1)} %bitcast.92, bf16[2,4096,384]{2,1,0:T(8,128)(2,1)} %param.10, f32[768,384]{1,0:T(8,128)S(1)} %copy-done.2), kind=kOutput, calls=%fused_computation.30 | convolution fusion | flops 2417688576 | bytes 11206656 | tf_op jit(solution)/shard_map/dot_general | solution.py:16
  218.5 5.5 %fusion.25 = bf16[768,384]{1,0:T(8,128)(2,1)S(1)} fusion(bf16[768,4096]{0,1:T(8,128)(2,1)S(1)} %bitcast.94, bf16[2,4096,384]{2,1,0:T(8,128)(2,1)} %param.10, f32[768,384]{1,0:T(8,128)S(1)} %fusion.6), kind=kOutput, calls=%fused_computation.29 | convolution fusion | flops 2417688576 | bytes 11206656 | tf_op jit(solution)/shard_map/dot_general | solution.py:16
  224.0 3.7 fusion
  227.7 3.7 fusion.1
  231.4 5.4 %pad_maximum_fusion = bf16[2,8,96,4096]{3,2,1,0:T(8,128)(2,1)} fusion(bf16[1,8,96,4096]{3,2,1,0:T(8,128)(2,1)S(1)} %fusion.1, bf16[1,8,96,4096]{3,2,1,0:T(8,128)(2,1)S(1)} %fusion), kind=kLoop, calls=%fused_computation.3 | loop fusion | flops 6291456 | bytes 25165824 | tf_op jit(solution)/shard_map/stack | solution.py:46
  236.8 97.3 %reduce-scatter.2.cloned.1.call-done = bf16[2,8,96,1024]{3,2,1,0:T(8,128)(2,1)} async-done(((bf16[2,8,96,4096]{3,2,1,0:T(8,128)(2,1)}), bf16[2,8,96,1024]{3,2,1,0:T(8,128)(2,1)}) %reduce-scatter.2.cloned.1.call-update) | async-done | bytes 3145744 | tf_op jit(solution)/shard_map/reduce_scatter | solution.py:48
  334.1 4.0 copy.28
  338.0 5.7 %all-to-all-start.1 = ((bf16[2,8,96,1024]{3,2,0,1:T(8,128)(2,1)}), bf16[2,8,96,1024]{3,2,0,1:T(8,128)(2,1)S(1)}, u32[]{:S(2)}, u32[]{:S(2)}) async-start(bf16[2,8,96,1024]{3,2,0,1:T(8,128)(2,1)} %copy.28), calls=%async_computation.2 | async-start | bytes 6291456 | tf_op jit(solution)/shard_map/all_to_all | solution.py:51
  343.8 70.4 %all-to-all-done.1 = bf16[2,8,96,1024]{3,2,0,1:T(8,128)(2,1)S(1)} async-done(((bf16[2,8,96,1024]{3,2,0,1:T(8,128)(2,1)}), bf16[2,8,96,1024]{3,2,0,1:T(8,128)(2,1)S(1)}, u32[]{:S(2)}, u32[]{:S(2)}) %all-to-all-start.1) | async-done | bytes 3145760 | tf_op jit(solution)/shard_map/all_to_all | solution.py:51
  414.2 3.4 bitcast_convert_fusion
  417.6 9.2 %gather_fusion.1 = f32[1024,1024]{1,0:T(8,128)} fusion(f32[1536,1024]{1,0:T(8,128)} %bitcast.86, s32[1024]{0:T(1024)S(1)} %broadcast_clamp_fusion), kind=kCustom, calls=%fused_computation.1 | custom fusion | bytes 8392704 | tf_op jit(solution)/shard_map/gather | solution.py:54
  426.9 4.2 fusion.2
  (43 shorter events, 3.9 us)
Async XLA Ops:
  6.5 143.0 %all-gather.5.cloned.1.call-start = ((), (), s32[]{:S(2)}) async-start(), calls=%async_computation.4 | async-start | bytes 7864320 | tf_op jit(solution)/shard_map/all_gather | solution.py:9
  104.0 93.5 %all-gather.7.cloned.1.call-start = ((), (), s32[]{:S(2)}) async-start(), calls=%async_computation.5 | async-start | bytes 7864320 | tf_op jit(solution)/shard_map/all_gather | solution.py:9
  104.7 229.4 %reduce-scatter.2.cloned.1.call-start = ((), (), s32[]{:S(2)}) async-start(), calls=%async_computation.3 | async-start | bytes 15728640 | tf_op jit(solution)/shard_map/reduce_scatter | solution.py:48
  197.5 15.4 %slice-start = ((s8[6291456]{0:T(1024)(128)(4,1)}), s8[2097152]{0:T(1024)(128)(4,1)S(1)}, s32[]{:S(2)}) async-start(s8[6291456]{0:T(1024)(128)(4,1)} %bitcast.90), calls=%async_computation.6 | async-start | bytes 4194304
  206.2 6.6 %slice-start.1 = ((s8[6291456]{0:T(1024)(128)(4,1)}), s8[4194304]{0:T(1024)(128)(4,1)S(1)}, s32[]{:S(2)}) async-start(s8[6291456]{0:T(1024)(128)(4,1)} %bitcast.90), calls=%async_computation.7 | async-start | bytes 8388608
  206.2 6.7 %copy-start.2 = (f32[768,384]{1,0:T(8,128)S(1)}, f32[768,384]{1,0:T(8,128)}, u32[]{:S(2)}) copy-start(f32[768,384]{1,0:T(8,128)} %fusion.11) | copy-start | bytes 3538948
  212.9 5.6 %copy-start = (bf16[4,1,768,1024]{2,3,0,1:T(8,128)(2,1)S(1)}, bf16[4,1,768,1024]{2,3,0,1:T(8,128)(2,1)}, u32[]{:S(2)}) copy-start(bf16[4,1,768,1024]{2,3,0,1:T(8,128)(2,1)} %copy.27) | copy-start | bytes 18874372
  212.9 11.1 %slice-start.2 = ((s8[6291456]{0:T(1024)(128)(4,1)}), s8[4194304]{0:T(1024)(128)(4,1)S(1)}, s32[]{:S(2)}) async-start(s8[6291456]{0:T(1024)(128)(4,1)} %bitcast.100), calls=%async_computation.8 | async-start | bytes 8388608
  218.4 5.6 %slice-start.3 = ((s8[6291456]{0:T(1024)(128)(4,1)}), s8[2097152]{0:T(1024)(128)(4,1)S(1)}, s32[]{:S(2)}) async-start(s8[6291456]{0:T(1024)(128)(4,1)} %bitcast.100), calls=%async_computation.9 | async-start | bytes 4194304
  338.0 5.7 %copy-start.1 = (f32[128,8]{0,1:T(8,128)S(1)}, f32[128,8]{0,1:T(8,128)}, u32[]{:S(2)}) copy-start(f32[128,8]{0,1:T(8,128)} %param.8) | copy-start | bytes 12292
  338.0 76.2 %all-to-all-start.1 = ((bf16[2,8,96,1024]{3,2,0,1:T(8,128)(2,1)}), bf16[2,8,96,1024]{3,2,0,1:T(8,128)(2,1)S(1)}, u32[]{:S(2)}, u32[]{:S(2)}) async-start(bf16[2,8,96,1024]{3,2,0,1:T(8,128)(2,1)} %copy.28), calls=%async_computation.2 | async-start | bytes 6291456 | tf_op jit(solution)/shard_map/all_to_all | solution.py:51
Sparse Core Ops, SparseCore 0:
  104.1 45.3 all-gather.4
  151.1 46.3 all-gather.6
  236.9 97.1 reduce-scatter.1
